TPU v7x, 32 devices: a whole 2x2x4 slice. The times are simulated.
32 devices in a mesh: groups: 2 (over y), gx: 4 (over z), gy: 2 (over x), gz: 2 (over core).
Axes of the slice: x: 2, y: 2, z: 4, core: 2. Of those that a mesh axis runs over, the one named last changes fastest.
Arguments:
- pair: float32 [256, 48, 48], P(('groups', 'gz'), 'gx', 'gy'), parts along dimension 0, may hold values from -6 to 6
- residue_mask: int32 [96], P('groups'), parts along dimension 0, may hold values 0 or 1
- norm_in_gain: float32 [2, 128], P(None, 'gz'), may hold values from 0.25 to 1.75
- proj_weight: bfloat16 [2, 4, 128, 128], P(None, None, None, 'gz'), may hold values from -0.5 to 0.5
- gate_weight: bfloat16 [2, 128, 128], P(None, None, 'gz'), may hold values from -0.5 to 0.5
- norm_out_gain: float32 [2, 128], P(None, 'gz'), may hold values from 0.25 to 1.75
- out_weight: bfloat16 [2, 128, 128], P(None, None, 'gz'), may hold values from -0.5 to 0.5
Outputs:
- pair_out: float32 [256, 48, 48], P(('groups', 'gz'), 'gx', 'gy'), parts along dimension 0
There are 2 independent parts, one for each index of `groups`. A program takes and returns all parts, laid end to end along the dimension named above; an argument that names none is the same for every part. Nothing has to cross between parts.
All inputs are finite; a program needn't handle non-finite values.
Results may differ from a plain program's by a relative error of at most 0.006.
Values may be sent and summed in bfloat16 or wider, within the bound.
A program may use at most 64 MiB of HBM per device.

v0:
```python
import jax
import jax.numpy as jnp
from jax import lax
from jax.sharding import PartitionSpec as P

EPSILON = 1e-05


def layer_norm_gathered(values, gain_part):
    full_values, full_gain = (
        lax.all_gather(values, "gz", axis=0, tiled=True),
        lax.all_gather(gain_part, "gz", axis=0, tiled=True),
    )
    mean_val = jnp.mean(full_values, axis=0)
    centred = full_values - mean_val
    spread = jnp.mean(centred * centred, axis=0)
    result = (centred * lax.rsqrt(spread + EPSILON) * full_gain[:, None, None]).astype(jnp.bfloat16)
    return result


def transpose_tile(pair_tile):
    depth_dim, tile_rows, tile_cols = pair_tile.shape
    across = lax.axis_size("gy")
    down_size = lax.axis_size("gx")
    quarter = tile_rows // across
    spread_rows = lax.all_to_all(pair_tile, "gy", split_axis=1, concat_axis=2, tiled=True)
    blocks = spread_rows.reshape(depth_dim, quarter, down_size, tile_rows)
    blocks = jnp.transpose(blocks, (0, 3, 2, 1))[:, :, :, None, :]
    moved_back = lax.all_to_all(
        lax.all_to_all(blocks, "gx", split_axis=2, concat_axis=2, tiled=True),
        "gy",
        split_axis=2,
        concat_axis=3,
        tiled=True,
    )
    return moved_back.reshape(depth_dim, tile_rows, tile_cols)


def fold_panels(left_tile, right_tile):
    left_panel = lax.all_gather(left_tile, "gy", axis=2, tiled=True)
    return jnp.einsum(
        "hik,hkj->hij",
        left_panel,
        lax.all_gather(right_tile, "gx", axis=1, tiled=True),
        preferred_element_type=jnp.float32,
    )


def per_device(
    pair, residue_mask, norm_in_gain, proj_weight, gate_weight, norm_out_gain, out_weight
):
    tile_rows = pair.shape[1]
    tile_cols = pair.shape[2]
    row_start = lax.axis_index("gx") * tile_rows
    col_start = lax.axis_index("gy") * tile_cols
    row_flags = lax.dynamic_slice_in_dim(residue_mask, row_start, tile_rows).astype(jnp.float32)
    col_flags = lax.dynamic_slice_in_dim(residue_mask, col_start, tile_cols).astype(jnp.float32)
    pair_mask = row_flags[:, None] * col_flags[None, :]
    current = pair
    for update in range(2):
        normed = layer_norm_gathered(current, norm_in_gain[update])
        projected = jnp.einsum(
            "cij,pch->phij", normed, proj_weight[update], preferred_element_type=jnp.float32
        )
        left_tile = (jax.nn.sigmoid(projected[0]) * projected[1] * pair_mask).astype(jnp.bfloat16)
        right_tile = (jax.nn.sigmoid(projected[2]) * projected[3] * pair_mask).astype(jnp.bfloat16)
        gate_values = jax.nn.sigmoid(
            jnp.einsum(
                "cij,cd->dij", normed, gate_weight[update], preferred_element_type=jnp.float32
            )
        )
        if update == 0:
            triangle = fold_panels(left_tile, transpose_tile(right_tile))
        else:
            triangle = fold_panels(transpose_tile(left_tile), right_tile)
        tri_normed = layer_norm_gathered(triangle, norm_out_gain[update])
        current = current + gate_values * jnp.einsum(
            "hij,hd->dij", tri_normed, out_weight[update], preferred_element_type=jnp.float32
        )
    return current


def solution(mesh):
    return jax.shard_map(
        per_device,
        mesh=mesh,
        in_specs=(
            P(("groups", "gz"), "gx", "gy"),
            P("groups"),
            P(None, "gz"),
            P(None, None, None, "gz"),
            P(None, None, "gz"),
            P(None, "gz"),
            P(None, None, "gz"),
        ),
        out_specs=P(("groups", "gz"), "gx", "gy"),
        check_vma=False,
    )
```

profile of v0, /device:TPU:0, one launch (start us, length us, event | category | flops | bytes accessed | tf_op | source)
XLA Modules:
  0.0 108.9 jit_solution(13316939528707844448)
XLA Ops:
  0.0 0.7 copy-done.7
  0.7 0.6 dynamic-slice
  1.9 0.7 copy-done.4
  2.7 0.1 bitcast_dynamic-update-slice_fusion.2
  2.8 0.7 copy-done.5
  3.5 0.1 bitcast_dynamic-update-slice_fusion.3
  3.6 1.2 %copy.59 = f32[64,12,24]{2,1,0:T(8,128)S(1)} copy(f32[64,12,24]{0,2,1:T(8,128)} %param.7) | data formatting | bytes 147456 | tf_op args[0]
  4.8 2.7 %all_gather.36 = f32[128,12,24]{2,1,0:T(8,128)S(1)} all-gather(f32[64,12,24]{2,1,0:T(8,128)S(1)} %copy.59), channel_id=1, replica_groups=mesh['groups'=2,'gx'=4,'gy'=2,'gz'=2] {'gz'}, dimensions={0}, use_global_device_ids=true | all-gather | bytes 221184 | tf_op jit(solution)/shard_map/all_gather | solution.py:11
  7.5 0.3 copy.60
  7.8 0.1 reduce_sum.72
  8.0 0.2 multiply_reduce_fusion.3
  8.2 0.6 copy-done.6
  9.1 2.5 %all-reduce.4 = (f32[128]{0:T(128)S(1)}, f32[128]{0:T(128)S(1)}, f32[128]{0:T(128)S(1)}, f32[128]{0:T(128)S(1)}) all-reduce(f32[128]{0:T(128)S(1)} %bitcast_dynamic-update-slice_fusion.3, f32[128]{0:T(128)S(1)} %bitcast_dynamic-update-slice_fusion.2, ...), channel_id=2, replica_groups=mesh['groups'=2,'gx'=4,'gy'=2,'gz'=2] {'gz'}, use_global_device_ids=true, to_apply=%add | all-reduce | flops 512 | bytes 4096
  11.6 0.3 convolution_bitcast_fusion.1
  11.8 0.1 fusion.26
  12.0 0.1 reshape.147
  12.1 7.8 %all_to_all.70 = bf16[2,2,4608]{2,1,0:T(2,128)(2,1)S(1)} all-to-all(bf16[2,2,4608]{2,1,0:T(2,128)(2,1)S(1)} %reshape.147), channel_id=1, replica_groups=mesh['groups'=2,'gx'=4,'gy'=2,'gz'=2] {'gy'}, dimensions={0} | all-to-all | bytes 73728 | tf_op jit(solution)/shard_map/all_to_all | solution.py:26
  19.9 0.1 reshape.148
  20.1 0.1 reshape.149
  20.2 10.3 %all_to_all.72 = bf16[4,2,2304]{2,1,0:T(2,128)(2,1)S(1)} all-to-all(bf16[4,2,2304]{2,1,0:T(2,128)(2,1)S(1)} %reshape.149), channel_id=1, replica_groups=mesh['groups'=2,'gx'=4,'gy'=2,'gz'=2] {'gx'}, dimensions={0} | all-to-all | bytes 73728 | tf_op jit(solution)/shard_map/all_to_all | solution.py:30
  30.6 0.1 reshape.150
  30.7 0.7 reshape.151
  31.4 3.3 %all-to-all-start.2 = ((bf16[2,2,4608]{2,1,0:T(2,128)(2,1)}), bf16[2,2,4608]{2,1,0:T(2,128)(2,1)S(1)}, u32[]{:S(2)}, u32[]{:S(2)}) async-start(bf16[2,2,4608]{2,1,0:T(2,128)(2,1)} %reshape.151), calls=%async_computation.2 | async-start | bytes 73728 | tf_op jit(solution)/shard_map/all_to_all | solution.py:29
  34.7 5.0 %all_gather.38 = bf16[64,12,48]{0,2,1:T(8,128)(2,1)S(1)} all-gather(bf16[64,12,24]{0,2,1:T(8,128)(2,1)S(1)} %get-tuple-element.12), channel_id=1, replica_groups=mesh['groups'=2,'gx'=4,'gy'=2,'gz'=2] {'gy'}, dimensions={2}, use_global_device_ids=true | all-gather | bytes 110592 | tf_op jit(solution)/shard_map/all_gather | solution.py:40
  39.7 0.3 copy.69
  40.0 0.1 reshape.152
  40.2 13.9 %all_gather.39 = bf16[64,48,24]{0,2,1:T(8,128)(2,1)S(1)} all-gather(bf16[64,12,24]{0,2,1:T(8,128)(2,1)S(1)} %reshape.104), channel_id=1, replica_groups=mesh['groups'=2,'gx'=4,'gy'=2,'gz'=2] {'gx'}, dimensions={1}, use_global_device_ids=true | all-gather | bytes 184320 | tf_op jit(solution)/shard_map/all_gather | solution.py:44
  54.1 0.6 copy.70
  54.8 0.3 fusion.62
  55.1 2.5 %all_gather.40 = f32[128,12,24]{2,1,0:T(8,128)S(1)} all-gather(f32[64,12,24]{2,1,0:T(8,128)S(1)} %fusion.62), channel_id=1, replica_groups=mesh['groups'=2,'gx'=4,'gy'=2,'gz'=2] {'gz'}, dimensions={0}, use_global_device_ids=true | all-gather | bytes 221184 | tf_op jit(solution)/shard_map/all_gather | solution.py:11
  57.7 0.3 copy.71
  58.0 0.1 reduce_sum.74
  58.1 0.2 multiply_reduce_fusion.2
  58.4 0.5 copy-done.2
  58.9 0.3 fusion.40
  59.2 0.6 copy-done
  59.8 0.3 fusion.6
  60.1 0.3 copy.72
  60.4 2.6 %all_gather.42 = f32[128,12,24]{2,1,0:T(8,128)S(1)} all-gather(f32[64,12,24]{2,1,0:T(8,128)S(1)} %copy.72), channel_id=1, replica_groups=mesh['groups'=2,'gx'=4,'gy'=2,'gz'=2] {'gz'}, dimensions={0}, use_global_device_ids=true | all-gather | bytes 221184 | tf_op jit(solution)/shard_map/all_gather | solution.py:11
  62.9 0.3 copy.73
  63.3 0.1 reduce_sum.76
  63.4 0.2 multiply_reduce_fusion.1
  63.6 0.3 convolution_bitcast_fusion
  63.9 0.1 fusion.14
  64.0 0.1 reshape.153
  64.2 7.3 %all_to_all.71 = bf16[2,2,4608]{2,1,0:T(2,128)(2,1)S(1)} all-to-all(bf16[2,2,4608]{2,1,0:T(2,128)(2,1)S(1)} %reshape.153), channel_id=1, replica_groups=mesh['groups'=2,'gx'=4,'gy'=2,'gz'=2] {'gy'}, dimensions={0} | all-to-all | bytes 73728 | tf_op jit(solution)/shard_map/all_to_all | solution.py:26
  71.5 0.1 reshape.154
  71.7 0.1 reshape.155
  71.8 8.0 %all_to_all.73 = bf16[4,2,2304]{2,1,0:T(2,128)(2,1)S(1)} all-to-all(bf16[4,2,2304]{2,1,0:T(2,128)(2,1)S(1)} %reshape.155), channel_id=1, replica_groups=mesh['groups'=2,'gx'=4,'gy'=2,'gz'=2] {'gx'}, dimensions={0} | all-to-all | bytes 73728 | tf_op jit(solution)/shard_map/all_to_all | solution.py:30
  79.8 0.1 reshape.156
  80.0 0.7 reshape.157
  80.7 3.3 %all-to-all-start.5 = ((bf16[2,2,4608]{2,1,0:T(2,128)(2,1)}), bf16[2,2,4608]{2,1,0:T(2,128)(2,1)S(1)}, u32[]{:S(2)}, u32[]{:S(2)}) async-start(bf16[2,2,4608]{2,1,0:T(2,128)(2,1)} %reshape.157), calls=%async_computation.5 | async-start | bytes 73728 | tf_op jit(solution)/shard_map/all_to_all | solution.py:29
  84.0 14.0 %all_gather.45 = bf16[64,48,24]{0,2,1:T(8,128)(2,1)S(1)} all-gather(bf16[64,12,24]{0,2,1:T(8,128)(2,1)S(1)} %get-tuple-element.9), channel_id=1, replica_groups=mesh['groups'=2,'gx'=4,'gy'=2,'gz'=2] {'gx'}, dimensions={1}, use_global_device_ids=true | all-gather | bytes 184320 | tf_op jit(solution)/shard_map/all_gather | solution.py:44
  98.0 0.6 copy.80
  98.6 0.1 reshape.158
  98.8 5.0 %all_gather.44 = bf16[64,12,48]{0,2,1:T(8,128)(2,1)S(1)} all-gather(bf16[64,12,24]{0,2,1:T(8,128)(2,1)S(1)} %reshape.106), channel_id=1, replica_groups=mesh['groups'=2,'gx'=4,'gy'=2,'gz'=2] {'gy'}, dimensions={2}, use_global_device_ids=true | all-gather | bytes 110592 | tf_op jit(solution)/shard_map/all_gather | solution.py:40
  103.9 0.3 copy.79
  104.1 0.3 fusion.63
  104.5 2.5 %all_gather.46 = f32[128,12,24]{2,1,0:T(8,128)S(1)} all-gather(f32[64,12,24]{2,1,0:T(8,128)S(1)} %fusion.63), channel_id=1, replica_groups=mesh['groups'=2,'gx'=4,'gy'=2,'gz'=2] {'gz'}, dimensions={0}, use_global_device_ids=true | all-gather | bytes 221184 | tf_op jit(solution)/shard_map/all_gather | solution.py:11
  107.0 0.3 copy.81
  107.3 0.1 reduce_sum.78
  107.5 0.2 multiply_reduce_fusion
  107.7 0.3 fusion.41
  108.0 1.0 fusion.11
  (43 shorter events, 0.8 us)
Async XLA Ops:
  0.0 0.7 copy-start.7
  1.9 0.7 copy-start.4
  2.8 0.7 copy-start.5
  7.9 3.6 %copy-start.1 = (bf16[2,4,128,64]{2,3,1,0:T(8,128)(2,1)S(1)}, bf16[2,4,128,64]{2,3,1,0:T(8,128)(2,1)}, u32[]{:S(2)}) copy-start(bf16[2,4,128,64]{2,3,1,0:T(8,128)(2,1)} %param.10) | copy-start | bytes 393220
  8.2 0.7 copy-start.6
  31.4 8.6 %all-to-all-start.2 = ((bf16[2,2,4608]{2,1,0:T(2,128)(2,1)}), bf16[2,2,4608]{2,1,0:T(2,128)(2,1)S(1)}, u32[]{:S(2)}, u32[]{:S(2)}) async-start(bf16[2,2,4608]{2,1,0:T(2,128)(2,1)} %reshape.151), calls=%async_computation.2 | async-start | bytes 73728 | tf_op jit(solution)/shard_map/all_to_all | solution.py:29
  58.1 0.8 copy-start.2
  58.9 0.9 copy-start
  58.9 0.9 copy-start.3
  80.7 17.9 %all-to-all-start.5 = ((bf16[2,2,4608]{2,1,0:T(2,128)(2,1)}), bf16[2,2,4608]{2,1,0:T(2,128)(2,1)S(1)}, u32[]{:S(2)}, u32[]{:S(2)}) async-start(bf16[2,2,4608]{2,1,0:T(2,128)(2,1)} %reshape.157), calls=%async_computation.5 | async-start | bytes 73728 | tf_op jit(solution)/shard_map/all_to_all | solution.py:29
where the time goes:
time: 110 us; the launch traced here: 109 us
  blocking collectives  84.3 us (77%)
  local copies, waits for them, and re-layouts  12.3 us (11%)
  starting transfers between devices  6.52 us (6%)
  matrix products  3.03 us (3%)
  other arithmetic  1.82 us (2%)
    all_gather x2, blocking collectives, fold_panels(): lax.all_gather(right_tile, 'gx', axis=1, tiled=True)  27.9 us
    all_to_all x2, blocking collectives, transpose_tile(): lax.all_to_all(blocks, 'gx', split_axis=2, concat_axis=2, tiled=True)  18.4 us
    all_to_all x2, blocking collectives, transpose_tile(): lax.all_to_all(pair_tile, 'gy', split_axis=1, concat_axis=2, tiled=True)  15.2 us
    all_gather x4, blocking collectives, layer_norm_gathered(): lax.all_gather(values, 'gz', axis=0, tiled=True)  10.3 us
    all_gather x2, blocking collectives, fold_panels(): left_panel = lax.all_gather(left_tile, 'gy', axis=2, tiled=True)  10 us
    unnamed x42, local copies, waits for them, and re-layouts  8.64 us
    all_to_all x2, starting transfers between devices, transpose_tile(): lax.all_to_all(lax.all_to_all(blocks, 'gx', split_axis=2, concat_axis=2,...  6.52 us
    unnamed x1, blocking collectives  2.48 us
  transfers between devices with their start and end apart: 2, of which 0 were waited for; matrix products, arithmetic and copies ran while one was open for 1% of the time, Pallas kernels for 0%

commit v1 on v0

--- a/solution.py
+++ b/solution.py
@@ -1,6 +1,10 @@
+import functools
+
 import jax
 import jax.numpy as jnp
 from jax import lax
+from jax.experimental import pallas as pl
+from jax.experimental.pallas import tpu as pltpu
 from jax.sharding import PartitionSpec as P
 
 EPSILON = 1e-05
@@ -80,9 +84,227 @@
     return current
 
 
+MESH_ID = pl.DeviceIdType.MESH
+
+
+def channel_norm(values, gain_row):
+    mean_val = jnp.mean(values, axis=1, keepdims=True)
+    centred = values - mean_val
+    spread = jnp.mean(centred * centred, axis=1, keepdims=True)
+    return (centred * lax.rsqrt(spread + EPSILON) * gain_row).astype(jnp.bfloat16)
+
+
+def rows_dot(rows, weight_t):
+    return lax.dot_general(
+        rows, weight_t, (((1,), (1,)), ((), ())), preferred_element_type=jnp.float32
+    )
+
+
+def fused_kernel(
+    sizes, x_ref, w_ref, g_ref, m_ref, o_ref,
+    x_all, w_all, g_in, l_send, r_send, l_got, r_got, l_wide, r_wide, turn_a, turn_b, z_t,
+    s_sem, x_sem, ls_sem, rs_sem, lr_sem, rr_sem, copy_sem,
+):
+    n_gx, n_gy, n_gz, side = sizes
+    n_q = n_gy * n_gz
+    row_id, gy_id, gz_id = lax.axis_index("gx"), lax.axis_index("gy"), lax.axis_index("gz")
+    col_id = gy_id * n_gz + gz_id
+    other = 1 - gz_id
+    half = w_ref.shape[2]
+    on_diag = row_id == col_id
+
+    def device(at_row, at_col):
+        return {"gx": at_row, "gy": at_col // n_gz, "gz": lax.rem(at_col, n_gz)}
+
+    barrier = pltpu.get_barrier_semaphore()
+    for step in range(1, n_gx * n_q):
+        peer = lax.rem(row_id * n_q + col_id + step, n_gx * n_q)
+        pl.semaphore_signal(
+            barrier, inc=1, device_id=device(peer // n_q, lax.rem(peer, n_q)), device_id_type=MESH_ID
+        )
+    own_w = pltpu.make_async_copy(w_ref, w_all.at[:, :, pl.ds(gz_id * half, half), :], copy_sem.at[0])
+    own_w.start()
+    pl.semaphore_wait(barrier, n_gx * n_q - 1)
+
+    def push(src, dst, send_sem, recv_sem, to):
+        return pltpu.make_async_remote_copy(
+            src_ref=src, dst_ref=dst, send_sem=send_sem, recv_sem=recv_sem,
+            device_id=to, device_id_type=MESH_ID,
+        )
+
+    mate = {"gz": other}
+    swaps = [push(x_ref.at[other], x_all.at[gz_id], s_sem.at[0], x_sem.at[0], mate),
+             push(g_ref, g_in, s_sem.at[1], x_sem.at[1], mate)]
+    for u in range(2):
+        swaps.append(
+            push(w_ref.at[u], w_all.at[u, :, pl.ds(gz_id * half, half), :], s_sem.at[2 + u], x_sem.at[2 + u], mate)
+        )
+    for swap in swaps:
+        swap.start()
+    x_all[gz_id] = x_ref[gz_id]
+    mask = m_ref[...]
+    own_w.wait()
+    swaps[0].wait()
+    swaps[1].wait()
+    gains = g_ref[...] + g_in[...]
+    current = jnp.transpose(x_all[...].reshape(2 * half, side * side), (1, 0))
+
+    for u in range(2):
+        swaps[2 + u].wait()
+        normed = channel_norm(current, gains[u : u + 1])
+        weights = w_all[u, 0:5].reshape(5 * 2 * half, 2 * half)
+        projected = rows_dot(normed, weights)
+        part = [projected[:, p * 2 * half : (p + 1) * 2 * half] for p in range(5)]
+        right = jax.nn.sigmoid(part[2]) * part[3] * mask
+        left = jax.nn.sigmoid(part[0]) * part[1] * mask
+        if u == 0:
+            turn_a[...] = right
+            for k in range(side):
+                turn_b[pl.ds(k * side, side), :] = turn_a[pl.ds(k, side, stride=side), :]
+            right = turn_b[...]
+        r_send[u] = right.astype(jnp.bfloat16)
+        l_send[u] = left.astype(jnp.bfloat16)
+        gate = jax.nn.sigmoid(part[4])
+        if u == 0:
+            block = col_id
+            wide_src, wide_dst = r_send.at[u], r_got.at[u, block]
+            wide_to = [device(t, row_id) for t in range(n_gx)]
+            wide_self = [on_diag & (row_id == t) for t in range(n_gx)]
+            wide_sems = (rs_sem, rr_sem)
+            near_src, near_dst = l_send.at[u], l_got.at[u, block]
+            near_sems = (ls_sem, lr_sem)
+            near_to = [device(row_id, lax.rem(col_id + t, n_q)) for t in range(1, n_q)]
+        else:
+            block = row_id
+            wide_src, wide_dst = l_send.at[u], l_got.at[u, block]
+            wide_to = [device(col_id, t) for t in range(n_q)]
+            wide_self = [on_diag & (col_id == t) for t in range(n_q)]
+            wide_sems = (ls_sem, lr_sem)
+            near_src, near_dst = r_send.at[u], r_got.at[u, block]
+            near_sems = (rs_sem, rr_sem)
+            near_to = [device(lax.rem(row_id + t, n_gx), col_id) for t in range(1, n_gx)]
+        sent = []
+        for t, to in enumerate(wide_to):
+            copy = push(wide_src, wide_dst, wide_sems[0].at[u, t], wide_sems[1].at[u, block], to)
+            guard = jnp.logical_not(wide_self[t])
+            pl.when(guard)(copy.start)
+            sent.append((guard, copy))
+        for t, to in enumerate(near_to):
+            copy = push(near_src, near_dst, near_sems[0].at[u, t], near_sems[1].at[u, block], to)
+            copy.start()
+            sent.append((None, copy))
+
+        totals = tuple(jnp.zeros((side, 2 * half), jnp.float32) for _ in range(side))
+        steps = n_q if u == 0 else n_gx
+        for t in range(steps):
+            slot = lax.rem(block + t, steps)
+            l_in = push(l_send.at[u], l_got.at[u, slot], ls_sem.at[u, 0], lr_sem.at[u, slot], mate)
+            r_in = push(r_send.at[u], r_got.at[u, slot], rs_sem.at[u, 0], rr_sem.at[u, slot], mate)
+            wide_in, near_in = (r_in, l_in) if u == 0 else (l_in, r_in)
+            wide_got, near_got = (r_got, l_got) if u == 0 else (l_got, r_got)
+            wide_mine, near_mine = (r_send, l_send) if u == 0 else (l_send, r_send)
+            if t == 0:
+                near_got[u, slot] = near_mine[u]
+
+                @pl.when(on_diag)
+                def _():
+                    wide_got[u, slot] = wide_mine[u]
+
+                pl.when(jnp.logical_not(on_diag))(wide_in.wait_recv)
+            else:
+                near_in.wait_recv()
+                wide_in.wait_recv()
+            l_wide[...] = l_got[u, slot].astype(jnp.float32)
+            r_wide[...] = r_got[u, slot].astype(jnp.float32)
+            fresh = list(totals)
+            for k in range(side):
+                right_k = r_wide[pl.ds(k * side, side), :]
+                for i in range(side):
+                    at = i * side + k if u == 0 else k * side + i
+                    fresh[i] = fresh[i] + l_wide[pl.ds(at, 1), :] * right_k
+            totals = tuple(fresh)
+        for i in range(side):
+            turn_a[pl.ds(i * side, side), :] = totals[i]
+        tri_normed = channel_norm(turn_a[...], gains[2 + u : 3 + u])
+        current = current + gate * rows_dot(tri_normed, w_all[u, 5])
+        for guard, copy in sent:
+            if guard is None:
+                copy.wait_send()
+            else:
+                pl.when(guard)(copy.wait_send)
+
+    z_t[...] = jnp.transpose(current, (1, 0)).reshape(2, half, side * side)
+    back = push(z_t.at[other], o_ref.at[gz_id], s_sem.at[4], x_sem.at[4], mate)
+    back.start()
+    o_ref[gz_id] = z_t[gz_id]
+    back.wait()
+
+
+def fused_device(
+    sizes, pair, residue_mask, norm_in_gain, proj_weight, gate_weight, norm_out_gain, out_weight
+):
+    n_gx, n_gy, n_gz, side = sizes
+    half = pair.shape[0]
+    full = 2 * half
+    pairs = side * side
+    n_q = n_gy * n_gz
+    gz_id = lax.axis_index("gz")
+    row_start = lax.axis_index("gx") * side
+    col_start = (lax.axis_index("gy") * n_gz + gz_id) * side
+    row_flags = lax.dynamic_slice_in_dim(residue_mask, row_start, side).astype(jnp.float32)
+    col_flags = lax.dynamic_slice_in_dim(residue_mask, col_start, side).astype(jnp.float32)
+    mask = (row_flags[:, None] * col_flags[None, :]).reshape(pairs, 1)
+    x = jnp.transpose(pair.reshape(half, side, n_gz, side), (2, 0, 1, 3)).reshape(n_gz, half, pairs)
+    w = jnp.concatenate([proj_weight, gate_weight[:, None], out_weight[:, None]], axis=1)
+    w = jnp.transpose(w, (0, 1, 3, 2))
+    g = lax.dynamic_update_slice(
+        jnp.zeros((8, full), jnp.float32),
+        jnp.concatenate([norm_in_gain, norm_out_gain], axis=0),
+        (0, gz_id * half),
+    )
+    vmem = pl.BlockSpec(memory_space=pltpu.VMEM)
+    dma = pltpu.SemaphoreType.DMA
+    blocks = pltpu.VMEM((2, n_q, pairs, full), jnp.bfloat16)
+    out = pl.pallas_call(
+        functools.partial(fused_kernel, sizes),
+        out_shape=jax.ShapeDtypeStruct((n_gz, half, pairs), jnp.float32),
+        in_specs=[vmem] * 4,
+        out_specs=vmem,
+        scratch_shapes=[
+            pltpu.VMEM((n_gz, half, pairs), jnp.float32),
+            pltpu.VMEM((2, 6, full, full), jnp.bfloat16),
+            pltpu.VMEM((8, full), jnp.float32),
+            pltpu.VMEM((2, pairs, full), jnp.bfloat16),
+            pltpu.VMEM((2, pairs, full), jnp.bfloat16),
+            blocks,
+            blocks,
+            pltpu.VMEM((pairs, full), jnp.float32),
+            pltpu.VMEM((pairs, full), jnp.float32),
+            pltpu.VMEM((pairs, full), jnp.float32),
+            pltpu.VMEM((pairs, full), jnp.float32),
+            pltpu.VMEM((n_gz, half, pairs), jnp.float32),
+            dma((5,)), dma((5,)),
+            dma((2, n_q)), dma((2, n_q)), dma((2, n_q)), dma((2, n_q)),
+            dma((1,)),
+        ],
+        compiler_params=pltpu.CompilerParams(collective_id=0, has_side_effects=True),
+    )(x, w, g, mask)
+    out = jnp.transpose(out.reshape(n_gz, half, side, side), (1, 2, 0, 3))
+    return out.reshape(half, side, n_gz * side)
+
+
 def solution(mesh):
+    n_gx, n_gy, n_gz = (mesh.shape[name] for name in ("gx", "gy", "gz"))
+
+    def step(pair, *rest):
+        _, rows, cols = pair.shape
+        square = n_gz == 2 and n_gx == n_gy * n_gz and cols == n_gz * rows
+        if square:
+            return fused_device((n_gx, n_gy, n_gz, rows), pair, *rest)
+        return per_device(pair, *rest)
+
     return jax.shard_map(
-        per_device,
+        step,
         mesh=mesh,
         in_specs=(
             P(("groups", "gz"), "gx", "gy"),

time: 110 us -> 33.7 us (0.31)
  blocking collectives: 84.3 us -> 0 us
  Pallas kernels: 0 us -> 26.9 us
  local copies, waits for them, and re-layouts: 12.3 us -> 4.24 us
  starting transfers between devices: 6.52 us -> 0 us
  matrix products: 3.03 us -> 0 us
    all_gather x8 -> x0, blocking collectives: 48.2 us -> none  [the longest x2 27.9 us: fold_panels(): lax.all_gather(right_tile, 'gx', axis=1, tiled=True)]
    all_to_all x4 -> x0, blocking collectives: 33.6 us -> none  [the longest x2 18.4 us: transpose_tile(): lax.all_to_all(blocks, 'gx', split_axis=2, concat_axis=2, tiled=True)]
    pallas_call x0 -> x1, Pallas kernels: none -> 26.9 us  [fused_device(): pl.pallas_call(functools.partial(fused_kernel, sizes), out_shape=jax.Shap...]
    unnamed x42 -> x10, local copies, waits for them, and re-layouts: 8.64 us -> 0.62 us
    all_to_all x2 -> x0, starting transfers between devices: 6.52 us -> none  [transpose_tile(): lax.all_to_all(lax.all_to_all(blocks, 'gx', split_axis=2, concat_axis=2,...]
    all_gather x8 -> x0, local copies, waits for them, and re-layouts: 3.05 us -> none  [the longest x4 1.32 us: layer_norm_gathered(): lax.all_gather(values, 'gz', axis=0, tiled=True)]
    dot_general x8 -> x0, matrix products: 3.03 us -> none  [the longest x2 1.25 us: per_device(): jnp.einsum('cij,cd->dij', normed, gate_weight[update], preferred_element_...]
    unnamed x1 -> x0, blocking collectives: 2.48 us -> none
  transfers between devices with their start and end apart: 2 -> 0, of which waited for: 0 -> 0; matrix products, arithmetic and copies ran while one was open for 1% -> 0% of each run, Pallas kernels for 0% -> 0%
where the time goes in v1:
time: 33.7 us; the launch traced here: 33.5 us
  Pallas kernels  26.9 us (80%)
  local copies, waits for them, and re-layouts  4.24 us (13%)
  other arithmetic  2.28 us (7%)
    pallas_call x1, Pallas kernels, fused_device(): pl.pallas_call(functools.partial(fused_kernel, sizes), out_shape=jax.Shap...  26.9 us
    pallas_call x1, local copies, waits for them, and re-layouts, fused_device(): pl.pallas_call(functools.partial(fused_kernel, sizes), out_shape=jax.Shap...  1.02 us
    convert_element_type x1, other arithmetic, fused_device(): lax.dynamic_slice_in_dim(residue_mask, row_start, side).astype(jnp.float32)  0.8 us
    reshape x1, local copies, waits for them, and re-layouts, fused_device(): jnp.transpose(pair.reshape(half, side, n_gz, side), (2, 0, 1, 3))  0.78 us
    mul x1, local copies, waits for them, and re-layouts, fused_device(): mask = (row_flags[:, None] * col_flags[None, :]).reshape(pairs, 1)  0.71 us
    concatenate x1, other arithmetic, fused_device(): jnp.concatenate([norm_in_gain, norm_out_gain], axis=0)  0.7 us
    transpose x1, other arithmetic, fused_device(): w = jnp.transpose(w, (0, 1, 3, 2))  0.69 us
    reshape x1, local copies, waits for them, and re-layouts, fused_device(): return out.reshape(half, side, n_gz * side)  0.67 us

profile of v1, /device:TPU:0, one launch (start us, length us, event | category | flops | bytes accessed | tf_op | source)
XLA Modules:
  0.0 33.5 jit_solution(9382953837709023803)
XLA Ops:
  0.0 0.0 copy-start
  0.0 0.8 %dynamic-slice_convert_fusion.1 = (f32[12]{0:T(128)S(1)}, f32[12]{0:T(128)S(1)}) fusion(s32[48]{0:T(128)} %param.8, s32[]{:T(128)S(6)} %select_n.10, s32[]{:T(128)S(6)} %select_n.11), kind=kLoop, calls=%fused_computation.4 | loop fusion | flops 24 | bytes 200 | tf_op jit(solution)/shard_map/convert_element_type | solution.py:254
  0.8 0.7 %pad_maximum_fusion = f32[4,64]{1,0:T(4,128)S(1)} fusion(f32[2,64]{1,0:T(2,128)} %param.12, f32[2,64]{1,0:T(2,128)} %param.9), kind=kLoop, calls=%fused_computation.2 | loop fusion | flops 256 | bytes 2048 | tf_op jit(solution)/shard_map/concatenate | solution.py:262
  1.5 0.3 dynamic_update_slice.3.g_ref
  1.8 0.0 copy-start.4
  1.9 0.1 broadcast_multiply_fusion
  1.9 0.5 %copy-done.4 = f32[8,128]{1,0:T(8,128)} copy-done((f32[8,128]{1,0:T(8,128)}, f32[8,128]{1,0:T(8,128)S(1)}, u32[]{:S(2)}) %copy-start.4) | copy-done | bytes 4120
  2.4 0.7 %mul.43.m_ref = f32[144,1]{1,0:T(8,128)} reshape(f32[12,12]{1,0:T(8,128)S(1)} %broadcast_multiply_fusion) | data formatting | bytes 1152 | tf_op jit(solution)/shard_map/mul | solution.py:256
  3.1 0.0 copy-done
  3.2 0.1 copy.10
  3.3 0.0 copy-start.1
  3.3 0.0 copy-start.2
  3.3 0.0 copy-start.3
  3.3 0.8 %copy.11.x_ref = f32[2,64,144]{2,1,0:T(8,128)} copy(f32[2,64,144]{1,0,2:T(2,128)S(1)} %bitcast.14) | data formatting | bytes 147456 | tf_op jit(solution)/shard_map/reshape | solution.py:257
  4.1 0.1 copy-done.1
  4.2 0.0 copy-done.2
  4.2 0.0 copy-done.3
  4.2 0.7 %maximum_bitcast_fusion.w_ref = bf16[2,6,64,128]{3,2,1,0:T(8,128)(2,1)} fusion(bf16[2,1,128,64]{2,3,1,0:T(8,128)(2,1)S(1)} %bitcast.16, bf16[2,1,128,64]{2,3,1,0:T(8,128)(2,1)S(1)} %bitcast.17, bf16[2,4,128,64]{2,3,1,0:T(8,128)(2,1)S(1)} %copy-done.1), kind=kLoop, calls=%fused_computation | loop fusion | flops 196608 | bytes 393216 | tf_op jit(solution)/shard_map/transpose | solution.py:259
  4.9 26.9 %shard_map.73 = f32[2,64,144]{2,1,0:T(8,128)} custom-call(f32[2,64,144]{2,1,0:T(8,128)} %copy.11.x_ref, bf16[2,6,64,128]{3,2,1,0:T(8,128)(2,1)} %maximum_bitcast_fusion.w_ref, f32[8,128]{1,0:T(8,128)} %copy-done.4, f32[144,1]{1,0:T(8,128)} %mul.43.m_ref), custom_call_target="tpu_custom_call" | custom-call | tf_op jit(solution)/shard_map/pallas_call | solution.py:268
  31.7 1.0 %copy.13 = f32[2,64,144]{1,0,2:T(2,128)S(1)} copy(f32[2,64,144]{2,1,0:T(8,128)} %shard_map.73) | data formatting | bytes 147456 | tf_op jit(solution)/shard_map/pallas_call | solution.py:268
  32.8 0.7 %reshape.40 = f32[64,12,24]{0,2,1:T(8,128)} reshape(f32[64,12,2,12]{0,3,2,1:T(8,128)S(1)} %copy.14) | data formatting | bytes 147456 | tf_op jit(solution)/shard_map/reshape | solution.py:293
  (3 shorter events, 0.0 us)
Async XLA Ops:
  0.0 3.1 %copy-start = (f32[64,12,24]{0,2,1:T(8,128)S(1)}, f32[64,12,24]{0,2,1:T(8,128)}, u32[]{:S(2)}) copy-start(f32[64,12,24]{0,2,1:T(8,128)} %param.7) | copy-start | bytes 221188
  1.8 0.6 %copy-start.4 = (f32[8,128]{1,0:T(8,128)}, f32[8,128]{1,0:T(8,128)S(1)}, u32[]{:S(2)}) copy-start(f32[8,128]{1,0:T(8,128)S(1)} %dynamic_update_slice.3.g_ref) | copy-start | bytes 12292
  3.3 0.9 %copy-start.1 = (bf16[2,4,128,64]{2,3,1,0:T(8,128)(2,1)S(1)}, bf16[2,4,128,64]{2,3,1,0:T(8,128)(2,1)}, u32[]{:S(2)}) copy-start(bf16[2,4,128,64]{2,3,1,0:T(8,128)(2,1)} %param.10) | copy-start | bytes 393220
  3.3 0.9 %copy-start.2 = (bf16[2,128,64]{1,2,0:T(8,128)(2,1)S(1)}, bf16[2,128,64]{1,2,0:T(8,128)(2,1)}, u32[]{:S(2)}) copy-start(bf16[2,128,64]{1,2,0:T(8,128)(2,1)} %param.13) | copy-start | bytes 98308
  3.3 0.9 %copy-start.3 = (bf16[2,128,64]{1,2,0:T(8,128)(2,1)S(1)}, bf16[2,128,64]{1,2,0:T(8,128)(2,1)}, u32[]{:S(2)}) copy-start(bf16[2,128,64]{1,2,0:T(8,128)(2,1)} %param.11) | copy-start | bytes 98308

commit v2 on v1

--- a/solution.py
+++ b/solution.py
@@ -101,8 +101,9 @@
 
 
 def fused_kernel(
-    sizes, x_ref, w_ref, g_ref, m_ref, o_ref,
-    x_all, w_all, g_in, l_send, r_send, l_got, r_got, l_wide, r_wide, turn_a, turn_b, z_t,
+    sizes, x_ref, mask_ref, gin_ref, proj_ref, gate_ref, gout_ref, outw_ref, o_ref,
+    x_in, x_out, x_got, p_all, g_all, d_all, gain_own, gain_got, l_send, r_send, l_got, r_got,
+    l_wide, r_wide, turn_a, turn_b, z_out, z_got,
     s_sem, x_sem, ls_sem, rs_sem, lr_sem, rr_sem, copy_sem,
 ):
     n_gx, n_gy, n_gz, side = sizes
@@ -110,51 +111,107 @@
     row_id, gy_id, gz_id = lax.axis_index("gx"), lax.axis_index("gy"), lax.axis_index("gz")
     col_id = gy_id * n_gz + gz_id
     other = 1 - gz_id
-    half = w_ref.shape[2]
+    half = x_ref.shape[2]
+    full = 2 * half
+    pairs = side * side
     on_diag = row_id == col_id
+    first = gz_id == 0
+    own_rows = pl.ds(pl.multiple_of(gz_id * half, half), half)
 
     def device(at_row, at_col):
         return {"gx": at_row, "gy": at_col // n_gz, "gz": lax.rem(at_col, n_gz)}
 
+    def push(src, dst, send_sem, recv_sem, to):
+        return pltpu.make_async_remote_copy(
+            src_ref=src, dst_ref=dst, send_sem=send_sem, recv_sem=recv_sem,
+            device_id=to, device_id_type=MESH_ID,
+        )
+
+    loads = [
+        pltpu.make_async_copy(src, dst, copy_sem.at[n])
+        for n, (src, dst) in enumerate((
+            (x_ref, x_in),
+            (proj_ref.at[0], p_all.at[0, :, own_rows, :]),
+            (gate_ref.at[0], g_all.at[0, own_rows, :]),
+            (outw_ref.at[0], d_all.at[0, own_rows, :]),
+            (proj_ref.at[1], p_all.at[1, :, own_rows, :]),
+            (gate_ref.at[1], g_all.at[1, own_rows, :]),
+            (outw_ref.at[1], d_all.at[1, own_rows, :]),
+        ))
+    ]
+    for load in loads:
+        load.start()
     barrier = pltpu.get_barrier_semaphore()
     for step in range(1, n_gx * n_q):
         peer = lax.rem(row_id * n_q + col_id + step, n_gx * n_q)
         pl.semaphore_signal(
             barrier, inc=1, device_id=device(peer // n_q, lax.rem(peer, n_q)), device_id_type=MESH_ID
         )
-    own_w = pltpu.make_async_copy(w_ref, w_all.at[:, :, pl.ds(gz_id * half, half), :], copy_sem.at[0])
-    own_w.start()
+
+    low_lanes = lax.broadcasted_iota(jnp.int32, (pairs, full), 1) < half
+    low_packed = low_lanes[: pairs // 2]
+
+    def pack(rows):
+        return jnp.where(low_packed, rows[: pairs // 2], pltpu.roll(rows[pairs // 2 :], half, 1))
+
+    def unpack(packed):
+        return jnp.concatenate([packed, pltpu.roll(packed, half, 1)], axis=0)
+
+    gain_own[...] = jnp.zeros_like(gain_own)
+    gain_own[0:2, 0:half] = gin_ref[...]
+    gain_own[2:4, 0:half] = gout_ref[...]
+    loads[0].wait()
+    turn_a[...] = jnp.zeros_like(turn_a)
+    turn_b[...] = jnp.zeros_like(turn_b)
+    for i in range(side):
+        left_cols, right_cols = x_in[i, 0:side, :], x_in[i, side : 2 * side, :]
+        turn_a[pl.ds(i * side, side), 0:half] = jnp.where(first, left_cols, right_cols)
+        turn_b[pl.ds(i * side, side), 0:half] = jnp.where(first, right_cols, left_cols)
+    x_out[...] = pack(turn_b[...])
+
+    n_res = mask_ref.shape[1]
+    pair_no = lax.broadcasted_iota(jnp.int32, (pairs, n_res), 0)
+    residue = lax.broadcasted_iota(jnp.int32, (pairs, n_res), 1)
+    in_row = ((pair_no.astype(jnp.float32) + 0.5) / side).astype(jnp.int32)
+    in_col = pair_no - in_row * side
+    flags = mask_ref[...].astype(jnp.float32)
+    row_flag = jnp.sum(jnp.where(residue == in_row + row_id * side, flags, 0.0), axis=1, keepdims=True)
+    col_flag = jnp.sum(jnp.where(residue == in_col + col_id * side, flags, 0.0), axis=1, keepdims=True)
+    mask = row_flag * col_flag
+
     pl.semaphore_wait(barrier, n_gx * n_q - 1)
-
-    def push(src, dst, send_sem, recv_sem, to):
-        return pltpu.make_async_remote_copy(
-            src_ref=src, dst_ref=dst, send_sem=send_sem, recv_sem=recv_sem,
-            device_id=to, device_id_type=MESH_ID,
-        )
-
     mate = {"gz": other}
-    swaps = [push(x_ref.at[other], x_all.at[gz_id], s_sem.at[0], x_sem.at[0], mate),
-             push(g_ref, g_in, s_sem.at[1], x_sem.at[1], mate)]
-    for u in range(2):
-        swaps.append(
-            push(w_ref.at[u], w_all.at[u, :, pl.ds(gz_id * half, half), :], s_sem.at[2 + u], x_sem.at[2 + u], mate)
-        )
+    swaps = [
+        push(src, dst, s_sem.at[n], x_sem.at[n], mate)
+        for n, (src, dst) in enumerate((
+            (x_out, x_got),
+            (gain_own, gain_got),
+            (proj_ref.at[0], p_all.at[0, :, own_rows, :]),
+            (gate_ref.at[0], g_all.at[0, own_rows, :]),
+            (outw_ref.at[0], d_all.at[0, own_rows, :]),
+            (proj_ref.at[1], p_all.at[1, :, own_rows, :]),
+            (gate_ref.at[1], g_all.at[1, own_rows, :]),
+            (outw_ref.at[1], d_all.at[1, own_rows, :]),
+        ))
+    ]
     for swap in swaps:
         swap.start()
-    x_all[gz_id] = x_ref[gz_id]
-    mask = m_ref[...]
-    own_w.wait()
     swaps[0].wait()
     swaps[1].wait()
-    gains = g_ref[...] + g_in[...]
-    current = jnp.transpose(x_all[...].reshape(2 * half, side * side), (1, 0))
+
+    def merge(mine, theirs, lanes):
+        low, high = jnp.where(first, mine, theirs), jnp.where(first, theirs, mine)
+        return jnp.where(lanes, low, pltpu.roll(high, half, 1))
+
+    gains = merge(gain_own[...], gain_got[...], low_lanes[0:8])
+    current = merge(turn_a[...], unpack(x_got[...]), low_lanes)
 
     for u in range(2):
-        swaps[2 + u].wait()
         normed = channel_norm(current, gains[u : u + 1])
-        weights = w_all[u, 0:5].reshape(5 * 2 * half, 2 * half)
-        projected = rows_dot(normed, weights)
-        part = [projected[:, p * 2 * half : (p + 1) * 2 * half] for p in range(5)]
+        loads[1 + 3 * u].wait()
+        swaps[2 + 3 * u].wait()
+        projected = rows_dot(normed, p_all[u].reshape(4 * full, full))
+        part = [projected[:, p * full : (p + 1) * full] for p in range(4)]
         right = jax.nn.sigmoid(part[2]) * part[3] * mask
         left = jax.nn.sigmoid(part[0]) * part[1] * mask
         if u == 0:
@@ -164,7 +221,6 @@
             right = turn_b[...]
         r_send[u] = right.astype(jnp.bfloat16)
         l_send[u] = left.astype(jnp.bfloat16)
-        gate = jax.nn.sigmoid(part[4])
         if u == 0:
             block = col_id
             wide_src, wide_dst = r_send.at[u], r_got.at[u, block]
@@ -194,7 +250,11 @@
             copy.start()
             sent.append((None, copy))
 
-        totals = tuple(jnp.zeros((side, 2 * half), jnp.float32) for _ in range(side))
+        for n in (1, 2):
+            loads[1 + 3 * u + n].wait()
+            swaps[2 + 3 * u + n].wait()
+        gate = jax.nn.sigmoid(rows_dot(normed, g_all[u]))
+        totals = tuple(jnp.zeros((side, full), jnp.float32) for _ in range(side))
         steps = n_q if u == 0 else n_gx
         for t in range(steps):
             slot = lax.rem(block + t, steps)
@@ -226,18 +286,24 @@
         for i in range(side):
             turn_a[pl.ds(i * side, side), :] = totals[i]
         tri_normed = channel_norm(turn_a[...], gains[2 + u : 3 + u])
-        current = current + gate * rows_dot(tri_normed, w_all[u, 5])
+        current = current + gate * rows_dot(tri_normed, d_all[u])
         for guard, copy in sent:
             if guard is None:
                 copy.wait_send()
             else:
                 pl.when(guard)(copy.wait_send)
 
-    z_t[...] = jnp.transpose(current, (1, 0)).reshape(2, half, side * side)
-    back = push(z_t.at[other], o_ref.at[gz_id], s_sem.at[4], x_sem.at[4], mate)
+    turned = pltpu.roll(current, half, 1)
+    z_out[...] = pack(jnp.where(first, turned, current))
+    back = push(z_out, z_got, s_sem.at[8], x_sem.at[8], mate)
     back.start()
-    o_ref[gz_id] = z_t[gz_id]
+    turn_a[...] = jnp.where(first, current, turned)
     back.wait()
+    turn_b[...] = unpack(z_got[...])
+    for i in range(side):
+        mine, theirs = turn_a[pl.ds(i * side, side), 0:half], turn_b[pl.ds(i * side, side), 0:half]
+        o_ref[i, 0:side, :] = jnp.where(first, mine, theirs)
+        o_ref[i, side : 2 * side, :] = jnp.where(first, theirs, mine)
 
 
 def fused_device(
@@ -248,49 +314,46 @@
     full = 2 * half
     pairs = side * side
     n_q = n_gy * n_gz
-    gz_id = lax.axis_index("gz")
-    row_start = lax.axis_index("gx") * side
-    col_start = (lax.axis_index("gy") * n_gz + gz_id) * side
-    row_flags = lax.dynamic_slice_in_dim(residue_mask, row_start, side).astype(jnp.float32)
-    col_flags = lax.dynamic_slice_in_dim(residue_mask, col_start, side).astype(jnp.float32)
-    mask = (row_flags[:, None] * col_flags[None, :]).reshape(pairs, 1)
-    x = jnp.transpose(pair.reshape(half, side, n_gz, side), (2, 0, 1, 3)).reshape(n_gz, half, pairs)
-    w = jnp.concatenate([proj_weight, gate_weight[:, None], out_weight[:, None]], axis=1)
-    w = jnp.transpose(w, (0, 1, 3, 2))
-    g = lax.dynamic_update_slice(
-        jnp.zeros((8, full), jnp.float32),
-        jnp.concatenate([norm_in_gain, norm_out_gain], axis=0),
-        (0, gz_id * half),
-    )
     vmem = pl.BlockSpec(memory_space=pltpu.VMEM)
+    hbm = pl.BlockSpec(memory_space=pl.ANY)
     dma = pltpu.SemaphoreType.DMA
     blocks = pltpu.VMEM((2, n_q, pairs, full), jnp.bfloat16)
+    block = pltpu.VMEM((pairs, full), jnp.float32)
+    packed = pltpu.VMEM((pairs // 2, full), jnp.float32)
     out = pl.pallas_call(
         functools.partial(fused_kernel, sizes),
-        out_shape=jax.ShapeDtypeStruct((n_gz, half, pairs), jnp.float32),
-        in_specs=[vmem] * 4,
+        out_shape=jax.ShapeDtypeStruct((side, n_gz * side, half), jnp.float32),
+        in_specs=[hbm, vmem, vmem, hbm, hbm, vmem, hbm],
         out_specs=vmem,
         scratch_shapes=[
-            pltpu.VMEM((n_gz, half, pairs), jnp.float32),
-            pltpu.VMEM((2, 6, full, full), jnp.bfloat16),
+            pltpu.VMEM((side, n_gz * side, half), jnp.float32),
+            packed,
+            packed,
+            pltpu.VMEM((2, 4, full, full), jnp.bfloat16),
+            pltpu.VMEM((2, full, full), jnp.bfloat16),
+            pltpu.VMEM((2, full, full), jnp.bfloat16),
+            pltpu.VMEM((8, full), jnp.float32),
             pltpu.VMEM((8, full), jnp.float32),
             pltpu.VMEM((2, pairs, full), jnp.bfloat16),
             pltpu.VMEM((2, pairs, full), jnp.bfloat16),
-            blocks,
-            blocks,
-            pltpu.VMEM((pairs, full), jnp.float32),
-            pltpu.VMEM((pairs, full), jnp.float32),
-            pltpu.VMEM((pairs, full), jnp.float32),
-            pltpu.VMEM((pairs, full), jnp.float32),
-            pltpu.VMEM((n_gz, half, pairs), jnp.float32),
-            dma((5,)), dma((5,)),
+            blocks, blocks,
+            block, block, block, block,
+            packed, packed,
+            dma((9,)), dma((9,)),
             dma((2, n_q)), dma((2, n_q)), dma((2, n_q)), dma((2, n_q)),
-            dma((1,)),
+            dma((7,)),
         ],
         compiler_params=pltpu.CompilerParams(collective_id=0, has_side_effects=True),
-    )(x, w, g, mask)
-    out = jnp.transpose(out.reshape(n_gz, half, side, side), (1, 2, 0, 3))
-    return out.reshape(half, side, n_gz * side)
+    )(
+        jnp.transpose(pair, (1, 2, 0)),
+        residue_mask[None, :],
+        norm_in_gain,
+        jnp.transpose(proj_weight, (0, 1, 3, 2)),
+        jnp.transpose(gate_weight, (0, 2, 1)),
+        norm_out_gain,
+        jnp.transpose(out_weight, (0, 2, 1)),
+    )
+    return jnp.transpose(out, (2, 0, 1))
 
 
 def solution(mesh):
@@ -298,7 +361,7 @@
 
     def step(pair, *rest):
         _, rows, cols = pair.shape
-        square = n_gz == 2 and n_gx == n_gy * n_gz and cols == n_gz * rows
+        square = n_gz == 2 and n_gx == n_gy * n_gz and cols == n_gz * rows and rows % 4 == 0
         if square:
             return fused_device((n_gx, n_gy, n_gz, rows), pair, *rest)
         return per_device(pair, *rest)

time: 33.7 us -> 28.6 us (0.85)
  local copies, waits for them, and re-layouts: 4.24 us -> 1.58 us
  other arithmetic: 2.28 us -> 0 us
    reshape x3 -> x0, local copies, waits for them, and re-layouts: 1.47 us -> none  [the longest x1 0.78 us: fused_device(): jnp.transpose(pair.reshape(half, side, n_gz, side), (2, 0, 1, 3))]
    pallas_call x1 -> x0, local copies, waits for them, and re-layouts: 1.02 us -> none  [fused_device(): pl.pallas_call(functools.partial(fused_kernel, sizes), out_shape=jax.Shap...]
    unnamed x10 -> x1, local copies, waits for them, and re-layouts: 0.62 us -> 1.58 us
    convert_element_type x1 -> x0, other arithmetic: 0.8 us -> none  [fused_device(): lax.dynamic_slice_in_dim(residue_mask, row_start, side).astype(jnp.float32)]
    mul x1 -> x0, local copies, waits for them, and re-layouts: 0.71 us -> none  [fused_device(): mask = (row_flags[:, None] * col_flags[None, :]).reshape(pairs, 1)]
    concatenate x1 -> x0, other arithmetic: 0.7 us -> none  [fused_device(): jnp.concatenate([norm_in_gain, norm_out_gain], axis=0)]
    transpose x1 -> x0, other arithmetic: 0.69 us -> none  [fused_device(): w = jnp.transpose(w, (0, 1, 3, 2))]
where the time goes in v2:
time: 28.6 us; the launch traced here: 28.5 us
  Pallas kernels  26.9 us (94%)
  local copies, waits for them, and re-layouts  1.58 us (6%)
    pallas_call x1, Pallas kernels, fused_device(): pl.pallas_call(functools.partial(fused_kernel, sizes), out_shape=jax.Shap...  26.9 us
    unnamed x1, local copies, waits for them, and re-layouts  1.58 us

profile of v2, /device:TPU:0, one launch (start us, length us, event | category | flops | bytes accessed | tf_op | source)
XLA Modules:
  0.0 28.5 jit_solution(8993763754262458385)
XLA Ops:
  0.0 26.9 %shard_map.73 = f32[12,24,64]{2,1,0:T(8,128)} custom-call(f32[12,24,64]{2,1,0:T(8,128)} %bitcast.7, s32[1,48]{1,0:T(1,128)} %bitcast.11, f32[2,64]{1,0:T(2,128)} %gin_ref.1, bf16[2,4,64,128]{3,2,1,0:T(8,128)(2,1)} %bitcast.8, bf16[2,64,128]{2,1,0:T(8,128)(2,1)} %bitcast.9, f32[2,64]{1,0:T(2,128)} %gout_ref.1, bf16[2,64,128]{2,1,0:T(8,128)(2,1)} %bitcast.10), custom_call_target="tpu_custom_call" | custom-call | tf_op jit(solution)/shard_map/pallas_call | solution.py:323
  26.9 1.6 %copy.9 = f32[64,12,24]{0,2,1:T(8,128)} copy(f32[64,12,24]{0,2,1:T(8,128)} %bitcast.6) | data formatting | bytes 147456

commit v3 on v2

--- a/solution.py
+++ b/solution.py
@@ -102,7 +102,7 @@
 
 def fused_kernel(
     sizes, x_ref, mask_ref, gin_ref, proj_ref, gate_ref, gout_ref, outw_ref, o_ref,
-    x_in, x_out, x_got, p_all, g_all, d_all, gain_own, gain_got, l_send, r_send, l_got, r_got,
+    x_in, x_out, x_got, p_all, g_all, d_all, gain_own, gain_got, l_send, r_send, part_send, l_got, r_got,
     l_wide, r_wide, turn_a, turn_b, z_out, z_got,
     s_sem, x_sem, ls_sem, rs_sem, lr_sem, rr_sem, copy_sem,
 ):
@@ -210,81 +210,104 @@
         normed = channel_norm(current, gains[u : u + 1])
         loads[1 + 3 * u].wait()
         swaps[2 + 3 * u].wait()
-        projected = rows_dot(normed, p_all[u].reshape(4 * full, full))
-        part = [projected[:, p * full : (p + 1) * full] for p in range(4)]
-        right = jax.nn.sigmoid(part[2]) * part[3] * mask
-        left = jax.nn.sigmoid(part[0]) * part[1] * mask
-        if u == 0:
-            turn_a[...] = right
-            for k in range(side):
-                turn_b[pl.ds(k * side, side), :] = turn_a[pl.ds(k, side, stride=side), :]
-            right = turn_b[...]
-        r_send[u] = right.astype(jnp.bfloat16)
-        l_send[u] = left.astype(jnp.bfloat16)
-        if u == 0:
-            block = col_id
-            wide_src, wide_dst = r_send.at[u], r_got.at[u, block]
-            wide_to = [device(t, row_id) for t in range(n_gx)]
-            wide_self = [on_diag & (row_id == t) for t in range(n_gx)]
-            wide_sems = (rs_sem, rr_sem)
-            near_src, near_dst = l_send.at[u], l_got.at[u, block]
-            near_sems = (ls_sem, lr_sem)
-            near_to = [device(row_id, lax.rem(col_id + t, n_q)) for t in range(1, n_q)]
-        else:
-            block = row_id
-            wide_src, wide_dst = l_send.at[u], l_got.at[u, block]
-            wide_to = [device(col_id, t) for t in range(n_q)]
-            wide_self = [on_diag & (col_id == t) for t in range(n_q)]
-            wide_sems = (ls_sem, lr_sem)
-            near_src, near_dst = r_send.at[u], r_got.at[u, block]
-            near_sems = (rs_sem, rr_sem)
-            near_to = [device(lax.rem(row_id + t, n_gx), col_id) for t in range(1, n_gx)]
-        sent = []
-        for t, to in enumerate(wide_to):
-            copy = push(wide_src, wide_dst, wide_sems[0].at[u, t], wide_sems[1].at[u, block], to)
-            guard = jnp.logical_not(wide_self[t])
-            pl.when(guard)(copy.start)
-            sent.append((guard, copy))
-        for t, to in enumerate(near_to):
-            copy = push(near_src, near_dst, near_sems[0].at[u, t], near_sems[1].at[u, block], to)
-            copy.start()
-            sent.append((None, copy))
-
-        for n in (1, 2):
-            loads[1 + 3 * u + n].wait()
-            swaps[2 + 3 * u + n].wait()
-        gate = jax.nn.sigmoid(rows_dot(normed, g_all[u]))
-        totals = tuple(jnp.zeros((side, full), jnp.float32) for _ in range(side))
-        steps = n_q if u == 0 else n_gx
-        for t in range(steps):
-            slot = lax.rem(block + t, steps)
-            l_in = push(l_send.at[u], l_got.at[u, slot], ls_sem.at[u, 0], lr_sem.at[u, slot], mate)
-            r_in = push(r_send.at[u], r_got.at[u, slot], rs_sem.at[u, 0], rr_sem.at[u, slot], mate)
-            wide_in, near_in = (r_in, l_in) if u == 0 else (l_in, r_in)
-            wide_got, near_got = (r_got, l_got) if u == 0 else (l_got, r_got)
-            wide_mine, near_mine = (r_send, l_send) if u == 0 else (l_send, r_send)
-            if t == 0:
-                near_got[u, slot] = near_mine[u]
-
-                @pl.when(on_diag)
-                def _():
-                    wide_got[u, slot] = wide_mine[u]
-
-                pl.when(jnp.logical_not(on_diag))(wide_in.wait_recv)
-            else:
-                near_in.wait_recv()
-                wide_in.wait_recv()
-            l_wide[...] = l_got[u, slot].astype(jnp.float32)
-            r_wide[...] = r_got[u, slot].astype(jnp.float32)
+        def gated(side_no):
+            projected = rows_dot(normed, p_all[u, 2 * side_no : 2 * side_no + 2].reshape(2 * full, full))
+            return jax.nn.sigmoid(projected[:, :full]) * projected[:, full:] * mask
+
+        def side_sends(what, targets):
+            src, dst, send_sems, recv_sems = what
+            for t, (to, guard) in enumerate(targets):
+                copy = push(src, dst, send_sems.at[u, t], recv_sems, to)
+                if guard is None:
+                    copy.start()
+                else:
+                    pl.when(guard)(copy.start)
+                sent.append((guard, copy))
+
+        def block_product(totals, left_row):
             fresh = list(totals)
             for k in range(side):
                 right_k = r_wide[pl.ds(k * side, side), :]
                 for i in range(side):
-                    at = i * side + k if u == 0 else k * side + i
-                    fresh[i] = fresh[i] + l_wide[pl.ds(at, 1), :] * right_k
-            totals = tuple(fresh)
-        for i in range(side):
-            turn_a[pl.ds(i * side, side), :] = totals[i]
+                    fresh[i] = fresh[i] + l_wide[pl.ds(left_row(k, i), 1), :] * right_k
+            return fresh
+
+        def late_weights():
+            for n in (1, 2):
+                loads[1 + 3 * u + n].wait()
+                swaps[2 + 3 * u + n].wait()
+            return jax.nn.sigmoid(rows_dot(normed, g_all[u]))
+
+        sent = []
+        plane = [
+            lax.rem(gy_id + t // n_gz, n_gy) * n_gz + lax.rem(gz_id + t, n_gz) for t in range(n_q)
+        ]
+        in_plane = [(device(row_id, at), None) for at in plane[:0:-1]]
+        zeros = [jnp.zeros((side, full), jnp.float32) for _ in range(side)]
+        if u == 0:
+            right_end = row_id >= n_gx // 2
+            far_rows = [jnp.where(right_end, t, n_gx - 1 - t) for t in range(n_gx)]
+            turn_a[...] = gated(1)
+            for k in range(side):
+                turn_b[pl.ds(k * side, side), :] = turn_a[pl.ds(k, side, stride=side), :]
+            r_send[...] = turn_b[...].astype(jnp.bfloat16)
+            side_sends(
+                (r_send, r_got.at[u, col_id], rs_sem, rr_sem.at[u, col_id]),
+                [(device(t, row_id), jnp.logical_not(on_diag & (row_id == t))) for t in far_rows],
+            )
+            l_send[u] = gated(0).astype(jnp.bfloat16)
+            side_sends((l_send.at[u], l_got.at[u, col_id], ls_sem, lr_sem.at[u, col_id]), in_plane)
+            gate = late_weights()
+            totals = zeros
+            for t, slot in enumerate(plane):
+                l_in = push(l_send.at[u], l_got.at[u, slot], ls_sem.at[u, 0], lr_sem.at[u, slot], mate)
+                r_in = push(r_send, r_got.at[u, slot], rs_sem.at[u, 0], rr_sem.at[u, slot], mate)
+                if t == 0:
+                    l_wide[...] = l_send[u].astype(jnp.float32)
+
+                    @pl.when(on_diag)
+                    def _():
+                        r_got[u, slot] = r_send[...]
+
+                    pl.when(jnp.logical_not(on_diag))(r_in.wait_recv)
+                else:
+                    l_in.wait_recv()
+                    r_in.wait_recv()
+                    l_wide[...] = l_got[u, slot].astype(jnp.float32)
+                r_wide[...] = r_got[u, slot].astype(jnp.float32)
+                totals = block_product(totals, lambda k, i: i * side + k)
+            for i in range(side):
+                turn_a[pl.ds(i * side, side), :] = totals[i]
+        else:
+            l_send[u] = gated(0).astype(jnp.bfloat16)
+            side_sends((l_send.at[u], l_got.at[u, col_id], ls_sem, lr_sem.at[u, col_id]), in_plane)
+            r_wide[...] = gated(1).astype(jnp.bfloat16).astype(jnp.float32)
+            gate = late_weights()
+            for t, slot in enumerate(plane):
+                if t == 0:
+                    l_wide[...] = l_send[u].astype(jnp.float32)
+                else:
+                    push(l_send.at[u], l_got.at[u, slot], ls_sem.at[u, 0], lr_sem.at[u, slot], mate).wait_recv()
+                    l_wide[...] = l_got[u, slot].astype(jnp.float32)
+                totals = block_product(zeros, lambda k, i: k * side + i)
+                for i in range(side):
+                    turn_b[pl.ds(i * side, side), :] = totals[i]
+                part_send[t] = turn_b[...].astype(jnp.bfloat16)
+
+                @pl.when(slot == row_id)
+                def _():
+                    turn_a[...] = turn_b[...]
+
+                copy = push(
+                    part_send.at[t], r_got.at[u, row_id], rs_sem.at[u, t], rr_sem.at[u, row_id],
+                    device(slot, col_id),
+                )
+                pl.when(slot != row_id)(copy.start)
+                sent.append((slot != row_id, copy))
+            for t in range(1, n_gx):
+                slot = lax.rem(row_id + t, n_gx)
+                push(part_send.at[0], r_got.at[u, slot], rs_sem.at[u, 0], rr_sem.at[u, slot], mate).wait_recv()
+                turn_a[...] += r_got[u, slot].astype(jnp.float32)
         tri_normed = channel_norm(turn_a[...], gains[2 + u : 3 + u])
         current = current + gate * rows_dot(tri_normed, d_all[u])
         for guard, copy in sent:
@@ -335,7 +358,8 @@
             pltpu.VMEM((8, full), jnp.float32),
             pltpu.VMEM((8, full), jnp.float32),
             pltpu.VMEM((2, pairs, full), jnp.bfloat16),
-            pltpu.VMEM((2, pairs, full), jnp.bfloat16),
+            pltpu.VMEM((pairs, full), jnp.bfloat16),
+            pltpu.VMEM((n_q, pairs, full), jnp.bfloat16),
             blocks, blocks,
             block, block, block, block,
             packed, packed,

time: 28.6 us -> 24.8 us (0.87)
  the two profiles are of different devices: /device:TPU:0 before, /device:TPU:3 now
where the time goes in v3:
time: 24.8 us; the launch traced here: 24.6 us
  Pallas kernels  23.1 us (93%)
  local copies, waits for them, and re-layouts  1.58 us (6%)
    pallas_call x1, Pallas kernels, fused_device(): pl.pallas_call(functools.partial(fused_kernel, sizes), out_shape=jax.Shap...  23.1 us
    unnamed x1, local copies, waits for them, and re-layouts  1.58 us

profile of v3, /device:TPU:3, one launch (start us, length us, event | category | flops | bytes accessed | tf_op | source)
XLA Modules:
  0.0 24.6 jit_solution(13482414268175434540)
XLA Ops:
  0.0 23.1 %shard_map.73 = f32[12,24,64]{2,1,0:T(8,128)} custom-call(f32[12,24,64]{2,1,0:T(8,128)} %bitcast.7, s32[1,48]{1,0:T(1,128)} %bitcast.11, f32[2,64]{1,0:T(2,128)} %gin_ref.1, bf16[2,4,64,128]{3,2,1,0:T(8,128)(2,1)} %bitcast.8, bf16[2,64,128]{2,1,0:T(8,128)(2,1)} %bitcast.9, f32[2,64]{1,0:T(2,128)} %gout_ref.1, bf16[2,64,128]{2,1,0:T(8,128)(2,1)} %bitcast.10), custom_call_target="tpu_custom_call" | custom-call | tf_op jit(solution)/shard_map/pallas_call | solution.py:346
  23.1 1.6 %copy.9 = f32[64,12,24]{0,2,1:T(8,128)} copy(f32[64,12,24]{0,2,1:T(8,128)} %bitcast.6) | data formatting | bytes 147456

commit v4 on v3

--- a/solution.py
+++ b/solution.py
@@ -103,7 +103,7 @@
 def fused_kernel(
     sizes, x_ref, mask_ref, gin_ref, proj_ref, gate_ref, gout_ref, outw_ref, o_ref,
     x_in, x_out, x_got, p_all, g_all, d_all, gain_own, gain_got, l_send, r_send, part_send, l_got, r_got,
-    l_wide, r_wide, turn_a, turn_b, z_out, z_got,
+    l_wide, r_wide, turn_a, turn_b, z_out, z_got, gin_own, gout_own, flag_own,
     s_sem, x_sem, ls_sem, rs_sem, lr_sem, rr_sem, copy_sem,
 ):
     n_gx, n_gy, n_gz, side = sizes
@@ -127,6 +127,12 @@
             device_id=to, device_id_type=MESH_ID,
         )
 
+    small = [
+        pltpu.make_async_copy(src, dst, copy_sem.at[n])
+        for n, (src, dst) in enumerate(((gin_ref, gin_own), (gout_ref, gout_own), (mask_ref, flag_own)), 7)
+    ]
+    for load in small:
+        load.start()
     loads = [
         pltpu.make_async_copy(src, dst, copy_sem.at[n])
         for n, (src, dst) in enumerate((
@@ -158,28 +164,20 @@
         return jnp.concatenate([packed, pltpu.roll(packed, half, 1)], axis=0)
 
     gain_own[...] = jnp.zeros_like(gain_own)
-    gain_own[0:2, 0:half] = gin_ref[...]
-    gain_own[2:4, 0:half] = gout_ref[...]
-    loads[0].wait()
-    turn_a[...] = jnp.zeros_like(turn_a)
-    turn_b[...] = jnp.zeros_like(turn_b)
-    for i in range(side):
-        left_cols, right_cols = x_in[i, 0:side, :], x_in[i, side : 2 * side, :]
-        turn_a[pl.ds(i * side, side), 0:half] = jnp.where(first, left_cols, right_cols)
-        turn_b[pl.ds(i * side, side), 0:half] = jnp.where(first, right_cols, left_cols)
-    x_out[...] = pack(turn_b[...])
-
+    for load in small:
+        load.wait()
+    gain_own[0:2, 0:half] = gin_own[...]
+    gain_own[2:4, 0:half] = gout_own[...]
     n_res = mask_ref.shape[1]
     pair_no = lax.broadcasted_iota(jnp.int32, (pairs, n_res), 0)
     residue = lax.broadcasted_iota(jnp.int32, (pairs, n_res), 1)
     in_row = ((pair_no.astype(jnp.float32) + 0.5) / side).astype(jnp.int32)
     in_col = pair_no - in_row * side
-    flags = mask_ref[...].astype(jnp.float32)
+    flags = flag_own[...].astype(jnp.float32)
     row_flag = jnp.sum(jnp.where(residue == in_row + row_id * side, flags, 0.0), axis=1, keepdims=True)
     col_flag = jnp.sum(jnp.where(residue == in_col + col_id * side, flags, 0.0), axis=1, keepdims=True)
     mask = row_flag * col_flag
 
-    pl.semaphore_wait(barrier, n_gx * n_q - 1)
     mate = {"gz": other}
     swaps = [
         push(src, dst, s_sem.at[n], x_sem.at[n], mate)
@@ -194,7 +192,20 @@
             (outw_ref.at[1], d_all.at[1, own_rows, :]),
         ))
     ]
-    for swap in swaps:
+    pl.semaphore_wait(barrier, n_gx * n_q - 1)
+    swaps[2].start()
+    swaps[1].start()
+    loads[0].wait()
+    turn_a[...] = jnp.zeros_like(turn_a)
+    turn_b[...] = jnp.zeros_like(turn_b)
+    for i in range(side):
+        left_cols, right_cols = x_in[i, 0:side, :], x_in[i, side : 2 * side, :]
+        turn_a[pl.ds(i * side, side), 0:half] = jnp.where(first, left_cols, right_cols)
+        turn_b[pl.ds(i * side, side), 0:half] = jnp.where(first, right_cols, left_cols)
+    x_out[...] = pack(turn_b[...])
+
+    swaps[0].start()
+    for swap in swaps[3:]:
         swap.start()
     swaps[0].wait()
     swaps[1].wait()
@@ -325,8 +336,11 @@
     turn_b[...] = unpack(z_got[...])
     for i in range(side):
         mine, theirs = turn_a[pl.ds(i * side, side), 0:half], turn_b[pl.ds(i * side, side), 0:half]
-        o_ref[i, 0:side, :] = jnp.where(first, mine, theirs)
-        o_ref[i, side : 2 * side, :] = jnp.where(first, theirs, mine)
+        x_in[i, 0:side, :] = jnp.where(first, mine, theirs)
+        x_in[i, side : 2 * side, :] = jnp.where(first, theirs, mine)
+    result = pltpu.make_async_copy(x_in, o_ref, copy_sem.at[0])
+    result.start()
+    result.wait()
 
 
 def fused_device(
@@ -337,7 +351,6 @@
     full = 2 * half
     pairs = side * side
     n_q = n_gy * n_gz
-    vmem = pl.BlockSpec(memory_space=pltpu.VMEM)
     hbm = pl.BlockSpec(memory_space=pl.ANY)
     dma = pltpu.SemaphoreType.DMA
     blocks = pltpu.VMEM((2, n_q, pairs, full), jnp.bfloat16)
@@ -346,8 +359,8 @@
     out = pl.pallas_call(
         functools.partial(fused_kernel, sizes),
         out_shape=jax.ShapeDtypeStruct((side, n_gz * side, half), jnp.float32),
-        in_specs=[hbm, vmem, vmem, hbm, hbm, vmem, hbm],
-        out_specs=vmem,
+        in_specs=[hbm] * 7,
+        out_specs=hbm,
         scratch_shapes=[
             pltpu.VMEM((side, n_gz * side, half), jnp.float32),
             packed,
@@ -363,9 +376,12 @@
             blocks, blocks,
             block, block, block, block,
             packed, packed,
+            pltpu.VMEM(norm_in_gain.shape, jnp.float32),
+            pltpu.VMEM(norm_out_gain.shape, jnp.float32),
+            pltpu.VMEM((1, residue_mask.shape[0]), jnp.int32),
             dma((9,)), dma((9,)),
             dma((2, n_q)), dma((2, n_q)), dma((2, n_q)), dma((2, n_q)),
-            dma((7,)),
+            dma((10,)),
         ],
         compiler_params=pltpu.CompilerParams(collective_id=0, has_side_effects=True),
     )(

time: 24.8 us -> 24.7 us (level)
  no operation moved by 1% of the time
where the time goes in v4:
time: 24.7 us; the launch traced here: 24.5 us
  Pallas kernels  22.9 us (93%)
  local copies, waits for them, and re-layouts  1.58 us (6%)
    pallas_call x1, Pallas kernels, fused_device(): pl.pallas_call(functools.partial(fused_kernel, sizes), out_shape=jax.Shap...  22.9 us
    unnamed x1, local copies, waits for them, and re-layouts  1.58 us

profile of v4, /device:TPU:3, one launch (start us, length us, event | category | flops | bytes accessed | tf_op | source)
XLA Modules:
  0.0 24.5 jit_solution(9481356455441228371)
XLA Ops:
  0.0 22.9 %shard_map.73 = f32[12,24,64]{2,1,0:T(8,128)} custom-call(f32[12,24,64]{2,1,0:T(8,128)} %bitcast.7, s32[1,48]{1,0:T(1,128)} %bitcast.11, f32[2,64]{1,0:T(2,128)} %gin_ref.1, bf16[2,4,64,128]{3,2,1,0:T(8,128)(2,1)} %bitcast.8, bf16[2,64,128]{2,1,0:T(8,128)(2,1)} %bitcast.9, f32[2,64]{1,0:T(2,128)} %gout_ref.1, bf16[2,64,128]{2,1,0:T(8,128)(2,1)} %bitcast.10), custom_call_target="tpu_custom_call" | custom-call | tf_op jit(solution)/shard_map/pallas_call | solution.py:359
  23.0 1.6 %copy.9 = f32[64,12,24]{0,2,1:T(8,128)} copy(f32[64,12,24]{0,2,1:T(8,128)} %bitcast.6) | data formatting | bytes 147456
